TPU v7x, 256 devices: a whole 4x4x8 slice. The times are simulated.
256 devices in a mesh: seq: 32 (over z, x_lo, core), fsdp: 8 (over x_hi, y).
Axes of the slice: x: 4 (x_hi: 2, x_lo: 2; x = x_hi * 2 + x_lo), y: 4, z: 8, core: 2. Of those that a mesh axis runs over, the one named last changes fastest.
Arguments:
- hidden_next: bfloat16 [8192, 8192], P('seq'), may hold values from -6 to 6
- values_next: bfloat16 [8192, 8192], P('seq', 'fsdp'), may hold values from -6 to 6
- seg_next: int32 [4], replicated, may hold values from 1 to 4096, 8192 in all
- proj_bc: bfloat16 [8192, 1024], P(('seq', 'fsdp')), may hold values from -0.09375 to 0.09375
- proj_dt: bfloat16 [8192, 128], P(('seq', 'fsdp')), may hold values from -0.0625 to 0.0625
- dt_bias: float32 [128], replicated, may hold values from -4 to -2.5
- decay_rate: float32 [128], replicated, may hold values from 0 to 1, as said below
- skip_gain: float32 [128], replicated, may hold values from 0.5 to 1.5
- bc_prev: bfloat16 [8192, 1024], P('seq'), may hold values from -4 to 4
- dt_prev: float32 [8192, 128], P('seq', 'fsdp'), may hold values from 0.01 to 0.3
- seg_prev: int32 [4], replicated, may hold values from 1 to 4096, 8192 in all
- grad_prev: bfloat16 [8192, 8192], P('seq', 'fsdp'), may hold values from -6 to 6
Outputs:
- out_next: bfloat16 [8192, 8192], P('seq', 'fsdp')
- grad_values: bfloat16 [8192, 8192], P('seq', 'fsdp')
Inputs may be any that keep to these rules, and one draw needn't show every extreme that they name: `seg_next`: lengths of the rollout's 4 segments in order, summing to 8192. `seg_prev`: lengths of the rollout's 4 segments in order, summing to 8192. `decay_rate`: positive.
All inputs are finite; a program needn't handle non-finite values.
Results may differ from a plain program's by a relative error of at most 0.0064.
Values may be sent and summed in bfloat16 or wider, within the bound.
A program may use at most 128 MiB of HBM per device.

v0:
```python
import jax
import jax.numpy as jnp
from jax import lax
from jax.sharding import Mesh
from jax.sharding import PartitionSpec as P

GW = 4
SPAN = 128
SEQ = ("seq_0", "seq_1", "seq_2")
SEQ_FSDP = ("seq_0", "seq_1", "seq_2", "fsdp")


def in_one_piece(arrays, axis, dim, along):
    widths = [a.shape[along] for a in arrays]
    both = jnp.concatenate(arrays, axis=along)
    whole = lax.all_gather(both, axis, axis=dim, tiled=True)
    return tuple(jnp.split(whole, [sum(widths[:k]) for k in range(1, len(widths))], axis=along))


def filled_with(array, identity):
    return jax.tree.map(
        lambda a, e: jnp.broadcast_to(jnp.asarray(e, a.dtype), a.shape), array, identity
    )


def prefix_by_axis(array, axes, combine, identity, reverse):
    before = start = filled_with(array, identity)
    so_far = array
    for axis in reversed(axes):
        size, index = (lax.axis_size(axis), lax.axis_index(axis))
        pieces = jax.tree.map(lambda part: lax.all_gather(part, axis), so_far)
        inside, so_far = (start, start)
        for k in reversed(range(size)) if reverse else range(size):
            passed = k > index if reverse else k < index
            so_far = combine(so_far, jax.tree.map(lambda part: part[k], pieces))
            inside = jax.tree.map(lambda new, old: jnp.where(passed, new, old), so_far, inside)
        before = combine(inside, before)
    return before


def joined(earlier, later):
    return (earlier[0] * later[0], later[0][:, None] * earlier[1] + later[1])


def segment_marks(lengths, offset, length):
    bounds = jnp.cumsum(lengths)[:-1]
    places = offset + jnp.arange(length + 1, dtype=jnp.int32) - 1
    return jnp.sum((bounds[None, :] <= places[:, None]).astype(jnp.int32), axis=1)


def pick_groups(bc_rows, first_group, groups_dev, nblocks):
    tokens_dev, width_all = bc_rows.shape
    state_dim = width_all // (2 * GW)
    halves = bc_rows.reshape(tokens_dev, 2, GW, state_dim)
    picked = lax.dynamic_slice_in_dim(halves, first_group, groups_dev, 2)
    b_vectors = picked[:, 0].reshape(nblocks, tokens_dev // nblocks, groups_dev, state_dim)
    c_vectors = picked[:, 1].reshape(nblocks, tokens_dev // nblocks, groups_dev, state_dim)
    return (b_vectors, c_vectors)


def block_parts(b_vectors, c_vectors, dt_blocks, marks_all, decay_local):
    nblocks, span_len, groups, state_dim = b_vectors.shape
    heads_dev = dt_blocks.shape[2]
    segment = marks_all[1:].reshape(nblocks, span_len)
    before = marks_all[:-1].reshape(nblocks, span_len)[:, 0]
    cumulative = jnp.cumsum(-dt_blocks * decay_local, axis=1)
    final_cum = cumulative[:, -1]
    places = jnp.arange(span_len)
    linked = (segment[:, :, None] == segment[:, None, :]) & (places[:, None] >= places[None, :])
    scores = jnp.einsum("ktgn,ksgn->kgts", c_vectors, b_vectors, preferred_element_type=jnp.float32)
    by_head = jnp.swapaxes(cumulative, 1, 2)
    spread = by_head[:, :, :, None] - by_head[:, :, None, :]
    decays = jnp.exp(jnp.where(linked[:, None], spread, -jnp.inf))
    weighted = (decays * jnp.swapaxes(dt_blocks, 1, 2)[:, :, None, :]).reshape(
        nblocks, groups, heads_dev // groups, span_len, span_len
    )
    mixing = (
        (weighted * scores[:, :, None])
        .reshape(nblocks, heads_dev, span_len, span_len)
        .astype(jnp.bfloat16)
    )
    keep_final = (segment == segment[:, -1:]).astype(jnp.float32)
    linked_in = (segment == before[:, None]).astype(jnp.float32)
    send_factor = keep_final[:, :, None] * jnp.exp(final_cum[:, None, :] - cumulative) * dt_blocks
    read_factor = linked_in[:, :, None] * jnp.exp(cumulative)
    carry_decay = (segment[:, -1] == before).astype(jnp.float32)[:, None] * jnp.exp(final_cum)
    return (mixing, send_factor, read_factor, carry_decay)


def outer_sum(values, vectors):
    nblocks, span_len, heads_dev, head_dim = values.shape
    groups = vectors.shape[2]
    grouped = values.reshape(nblocks, span_len, groups, heads_dev // groups, head_dim)
    result = jnp.einsum("ksgqp,ksgn->kgqpn", grouped, vectors, preferred_element_type=jnp.float32)
    return result.reshape(nblocks, heads_dev, head_dim * vectors.shape[3])


def read_state(state_now, vectors, factor):
    nblocks, heads_dev, head_dim, state_dim = state_now.shape
    groups = vectors.shape[2]
    grouped = state_now.reshape(nblocks, groups, heads_dev // groups, head_dim, state_dim)
    result = jnp.einsum(
        "kgqpn,ktgn->ktgqp", grouped, vectors.astype(jnp.float32), precision=lax.Precision.HIGHEST
    )
    return result.reshape(nblocks, vectors.shape[1], heads_dev, head_dim) * factor[:, :, :, None]


def body(
    hidden_next,
    values_next,
    seg_next,
    proj_bc,
    proj_dt,
    dt_bias,
    decay_rate,
    skip_gain,
    bc_prev,
    dt_prev,
    seg_prev,
    grad_prev,
):
    tokens_dev = hidden_next.shape[0]
    bc_width = proj_bc.shape[1]
    heads_all = proj_dt.shape[1]
    fsdp_count = lax.axis_size("fsdp")
    fsdp_place = lax.axis_index("fsdp")
    heads_dev = heads_all // fsdp_count
    head_dim = values_next.shape[1] // heads_dev
    state_dim = bc_width // (2 * GW)
    flat_size = head_dim * state_dim
    per_group = heads_all // GW
    groups_dev = max(1, heads_dev // per_group)
    first_head = fsdp_place * heads_dev
    first_group = first_head // per_group
    rows_dev = proj_bc.shape[0]
    seq_count = lax.axis_size(SEQ)
    arranged = hidden_next.reshape(tokens_dev, seq_count, fsdp_count, rows_dev)
    owned = lax.dynamic_slice_in_dim(arranged, fsdp_place, 1, 2).reshape(
        tokens_dev, seq_count * rows_dev
    )
    pieces = in_one_piece((proj_bc, proj_dt), SEQ, 0, 1)
    bc_sum, dt_sum = lax.psum(
        (
            jnp.dot(owned, pieces[0], preferred_element_type=jnp.float32),
            jnp.dot(owned, pieces[1], preferred_element_type=jnp.float32),
        ),
        "fsdp",
    )
    bc_next = bc_sum.astype(jnp.bfloat16)
    bias_local = lax.dynamic_slice_in_dim(dt_bias, first_head, heads_dev, 0)
    decay_local = lax.dynamic_slice_in_dim(decay_rate, first_head, heads_dev, 0)
    skip_local = lax.dynamic_slice_in_dim(skip_gain, first_head, heads_dev, 0)
    dt_next = jax.nn.softplus(
        lax.dynamic_slice_in_dim(dt_sum, first_head, heads_dev, 1) + bias_local
    )
    offset = lax.axis_index(SEQ) * tokens_dev
    nblocks = tokens_dev // SPAN
    unit_decay = jnp.ones((heads_dev,), jnp.float32)
    zero_state = jnp.zeros((heads_dev, flat_size), jnp.float32)
    inputs = values_next.reshape(nblocks, SPAN, heads_dev, head_dim)
    marks_next = segment_marks(seg_next, offset, tokens_dev)
    b_vectors, c_vectors = pick_groups(bc_next, first_group, groups_dev, nblocks)
    mixing, send_factor, read_factor, carry_decay = block_parts(
        b_vectors, c_vectors, dt_next.reshape(nblocks, SPAN, heads_dev), marks_next, decay_local
    )
    scaled = (inputs.astype(jnp.float32) * send_factor[:, :, :, None]).astype(jnp.bfloat16)
    local_sums = outer_sum(scaled, b_vectors)
    summary = (unit_decay, zero_state)
    for block_id in range(nblocks):
        summary = joined(summary, (carry_decay[block_id], local_sums[block_id]))
    arrived = prefix_by_axis((summary[0], summary[1]), SEQ, joined, (unit_decay, zero_state), False)
    state_now = arrived[1]
    starts_list = []
    for block_id in range(nblocks):
        starts_list.append(state_now)
        if block_id + 1 < nblocks:
            state_now = carry_decay[block_id][:, None] * state_now + local_sums[block_id]
    entering = jnp.stack(starts_list).reshape(nblocks, heads_dev, head_dim, state_dim)
    inside = jnp.einsum("khts,kshp->kthp", mixing, inputs, preferred_element_type=jnp.float32)
    output = (
        inside
        + read_state(entering, c_vectors, read_factor)
        + skip_local[:, None] * inputs.astype(jnp.float32)
    )
    out_next = output.astype(jnp.bfloat16).reshape(tokens_dev, heads_dev * head_dim)
    grads_in = grad_prev.reshape(nblocks, SPAN, heads_dev, head_dim)
    marks_prev = segment_marks(seg_prev, offset, tokens_dev)
    b_back, c_back = pick_groups(bc_prev, first_group, groups_dev, nblocks)
    mixing_back, send_back, read_back, carry_back = block_parts(
        b_back, c_back, dt_prev.reshape(nblocks, SPAN, heads_dev), marks_prev, decay_local
    )
    scaled_back = (grads_in.astype(jnp.float32) * read_back[:, :, :, None]).astype(jnp.bfloat16)
    local_back = outer_sum(scaled_back, c_back)
    summary_back = (unit_decay, zero_state)
    for block_id in reversed(range(nblocks)):
        summary_back = joined(summary_back, (carry_back[block_id], local_back[block_id]))
    arrived_back = prefix_by_axis(
        (summary_back[0], summary_back[1]), SEQ, joined, (unit_decay, zero_state), True
    )
    state_back = arrived_back[1]
    ends_list = [zero_state] * nblocks
    for block_id in reversed(range(nblocks)):
        ends_list[block_id] = state_back
        if block_id > 0:
            state_back = carry_back[block_id][:, None] * state_back + local_back[block_id]
    leaving = jnp.stack(ends_list).reshape(nblocks, heads_dev, head_dim, state_dim)
    inside_back = jnp.einsum(
        "khts,kthp->kshp", mixing_back, grads_in, preferred_element_type=jnp.float32
    )
    gradient = (
        inside_back
        + read_state(leaving, b_back, send_back)
        + skip_local[:, None] * grads_in.astype(jnp.float32)
    )
    grad_values = gradient.astype(jnp.bfloat16).reshape(tokens_dev, heads_dev * head_dim)
    return (out_next, grad_values)


def solution(mesh):
    split = Mesh(
        mesh.devices.reshape(8, 2, 2, mesh.shape["fsdp"]), ("seq_0", "seq_1", "seq_2", "fsdp")
    )
    in_specs = (
        P(SEQ, None),
        P(SEQ, "fsdp"),
        P(),
        P(SEQ_FSDP, None),
        P(SEQ_FSDP, None),
        P(),
        P(),
        P(),
        P(SEQ, None),
        P(SEQ, "fsdp"),
        P(),
        P(SEQ, "fsdp"),
    )
    out_specs = (P(SEQ, "fsdp"), P(SEQ, "fsdp"))
    return jax.shard_map(body, mesh=split, in_specs=in_specs, out_specs=out_specs, check_vma=False)
```

profile of v0, /device:TPU:1, one launch (start us, length us, event | category | flops | bytes accessed | tf_op | source)
XLA Modules:
  0.0 394.7 jit_solution(7305835161646682125)
XLA Ops:
  10.5 6.5 %copy.114 = bf16[256,8192]{0,1:T(8,128)(2,1)} copy(bf16[256,8192]{1,0:T(8,128)(2,1)} %param.12) | data formatting | bytes 8388608 | tf_op args[0]
  24.6 54.7 %all-gather.14.cloned.1.call-done = bf16[1024,1152]{1,0:T(8,128)(2,1)} async-done(((bf16[32,1152]{1,0:T(8,128)(2,1)}), bf16[1024,1152]{1,0:T(8,128)(2,1)}) %all-gather.14.cloned.1.call-update) | async-done | bytes 2359312 | tf_op jit(solution)/shard_map/all_gather | solution.py:16
  81.3 2.3 fusion
  83.6 67.7 %all-reduce.4 = bf16[256,1024]{1,0:T(8,128)(2,1)S(1)} all-reduce(f32[256,1024]{1,0:T(8,128)S(1)} %fusion), channel_id=1, replica_groups=mesh['seq_0'=8,'seq_1'=2,'seq_2'=2,'fsdp'=8] {'fsdp'}, use_global_device_ids=true, to_apply=%region_4.5 | all-reduce | flops 262144 | bytes 1572864 | tf_op jit(solution)/shard_map/psum | solution.py:142
  153.0 13.6 %all-reduce.3.cloned.1.call-done = f32[256,128]{0,1:T(8,128)} async-done(((f32[256,128]{0,1:T(8,128)}), f32[256,128]{0,1:T(8,128)}) %all-reduce.3.cloned.1.call-update) | async-done | bytes 131088 | tf_op jit(solution)/shard_map/psum | solution.py:142
  172.2 7.2 %all-gather.3 = f32[2,1,16]{2,1,0:T(1,128)S(1)} all-gather(f32[1,1,16]{2,1,0:T(1,128)S(1)} %get-tuple-element.64), channel_id=1, replica_groups=mesh['seq_0'=8,'seq_1'=2,'seq_2'=2,'fsdp'=8] {'seq_2'}, dimensions={0}, use_global_device_ids=true | all-gather | bytes 192 | tf_op jit(solution)/shard_map/all_gather | solution.py:31
  179.9 3.1 all-gather.4
  185.1 3.1 all-gather
  188.2 3.1 all-gather.1
  194.0 2.1 slice_add_fusion.10
  196.2 12.1 %all-gather.16.cloned.1.call-done = f32[2,16,8192]{2,1,0:T(8,128)} async-done(((f32[1,16,8192]{2,1,0:T(8,128)}), f32[2,16,8192]{2,1,0:T(8,128)}) %all-gather.16.cloned.1.call-update) | async-done | bytes 1048592 | tf_op jit(solution)/shard_map/all_gather | solution.py:31
  208.3 2.1 slice_add_fusion.22
  210.5 26.8 %all-gather.24.cloned.1.call-done = f32[2,16,8192]{2,1,0:T(8,128)} async-done(((f32[1,16,8192]{2,1,0:T(8,128)}), f32[2,16,8192]{2,1,0:T(8,128)}) %all-gather.24.cloned.1.call-update) | async-done | bytes 1048592 | tf_op jit(solution)/shard_map/all_gather | solution.py:31
  237.4 2.2 slice_add_fusion.8
  239.7 27.3 %all-gather.18.cloned.1.call-done = f32[2,16,8192]{2,1,0:T(8,128)} async-done(((f32[1,16,8192]{2,1,0:T(8,128)}), f32[2,16,8192]{2,1,0:T(8,128)}) %all-gather.18.cloned.1.call-update) | async-done | bytes 1048592 | tf_op jit(solution)/shard_map/all_gather | solution.py:31
  266.9 2.1 slice_add_fusion.20
  273.8 13.9 %all-gather.5 = f32[8,1,16]{2,1,0:T(1,128)S(1)} all-gather(f32[1,1,16]{2,1,0:T(1,128)S(1)} %copy-done.55), channel_id=1, replica_groups=mesh['seq_0'=8,'seq_1'=2,'seq_2'=2,'fsdp'=8] {'seq_0'}, dimensions={0}, use_global_device_ids=true | all-gather | bytes 576 | tf_op jit(solution)/shard_map/all_gather | solution.py:31
  287.7 12.6 %all-gather.2 = f32[8,1,16]{2,1,0:T(1,128)S(1)} all-gather(f32[1,1,16]{2,1,0:T(1,128)S(1)} %get-tuple-element.67), channel_id=1, replica_groups=mesh['seq_0'=8,'seq_1'=2,'seq_2'=2,'fsdp'=8] {'seq_0'}, dimensions={0}, use_global_device_ids=true | all-gather | bytes 576 | tf_op jit(solution)/shard_map/all_gather | solution.py:31
  302.2 2.7 convolution_bitcast_fusion.1
  304.9 19.6 %all-gather.26.cloned.1.call-done = f32[8,16,8192]{2,1,0:T(8,128)} async-done(((f32[1,16,8192]{2,1,0:T(8,128)}), f32[8,16,8192]{2,1,0:T(8,128)}) %all-gather.26.cloned.1.call-update) | async-done | bytes 4194320 | tf_op jit(solution)/shard_map/all_gather | solution.py:31
  324.6 3.2 add_bitcast_fusion
  331.6 2.6 reshape.987
  334.2 46.1 %all-gather.20.cloned.1.call-done = f32[8,16,8192]{2,1,0:T(8,128)} async-done(((f32[1,16,8192]{2,1,0:T(8,128)}), f32[8,16,8192]{2,1,0:T(8,128)}) %all-gather.20.cloned.1.call-update) | async-done | bytes 4194320 | tf_op jit(solution)/shard_map/all_gather | solution.py:31
  380.3 3.2 add_bitcast_fusion.1
  (225 shorter events, 39.8 us)
Async XLA Ops:
  7.2 72.2 %all-gather.14.cloned.1.call-start = ((), (), s32[]{:S(2)}) async-start(), calls=%async_computation | async-start | bytes 2433024 | tf_op jit(solution)/shard_map/all_gather | solution.py:16
  8.7 157.9 %all-reduce.3.cloned.1.call-start = ((), (), s32[]{:S(2)}) async-start(), calls=%async_computation.1 | async-start | bytes 262144 | tf_op jit(solution)/shard_map/psum | solution.py:142
  81.2 112.8 %all-gather.22.cloned.1.call-start = ((), (), s32[]{:S(2)}) async-start(), calls=%async_computation.5 | async-start | bytes 1572864 | tf_op jit(solution)/shard_map/all_gather | solution.py:31
  172.1 36.2 %all-gather.16.cloned.1.call-start = ((), (), s32[]{:S(2)}) async-start(), calls=%async_computation.2 | async-start | bytes 1572864 | tf_op jit(solution)/shard_map/all_gather | solution.py:31
  192.8 44.5 %all-gather.24.cloned.1.call-start = ((), (), s32[]{:S(2)}) async-start(), calls=%async_computation.6 | async-start | bytes 1572864 | tf_op jit(solution)/shard_map/all_gather | solution.py:31
  193.5 43.9 %copy-start.30 = (f32[16]{0:T(128)}, f32[16]{0:T(128)S(1)}, u32[]{:S(2)}) copy-start(f32[16]{0:T(128)S(1)} %get-tuple-element.61) | copy-start | bytes 196
  194.0 72.9 %copy-start.26 = (f32[16]{0:T(128)}, f32[16]{0:T(128)S(1)}, u32[]{:S(2)}) copy-start(f32[16]{0:T(128)S(1)} %get-tuple-element.70) | copy-start | bytes 196
  194.0 43.3 %copy-start.36 = (f32[16]{0:T(128)S(1)}, f32[16]{0:T(128)}, u32[]{:S(2)}) copy-start(f32[16]{0:T(128)} %get-tuple-element.59) | copy-start | bytes 196
  196.2 70.8 %all-gather.18.cloned.1.call-start = ((), (), s32[]{:S(2)}) async-start(), calls=%async_computation.3 | async-start | bytes 1572864 | tf_op jit(solution)/shard_map/all_gather | solution.py:31
  210.5 114.1 %all-gather.26.cloned.1.call-start = ((), (), s32[]{:S(2)}) async-start(), calls=%async_computation.7 | async-start | bytes 4718592 | tf_op jit(solution)/shard_map/all_gather | solution.py:31
  237.4 33.2 %copy-start.11 = (bf16[256,1,1,128]{3,2,1,0:T(2,128)(2,1)S(1)}, bf16[256,1,1,128]{3,2,1,0:T(2,128)(2,1)}, u32[]{:S(2)}) copy-start(bf16[256,1,1,128]{3,2,1,0:T(2,128)(2,1)} %get-tuple-element.24) | copy-start | bytes 196612
  237.4 33.2 %copy-start.10 = (bf16[256,1,1,128]{3,2,1,0:T(2,128)(2,1)S(1)}, bf16[256,1,1,128]{3,2,1,0:T(2,128)(2,1)}, u32[]{:S(2)}) copy-start(bf16[256,1,1,128]{3,2,1,0:T(2,128)(2,1)} %get-tuple-element.82) | copy-start | bytes 196612
  237.4 33.3 %copy-start.5 = (bf16[256,1,1,128]{3,0,2,1:T(8,128)(2,1)S(1)}, bf16[256,1,1,128]{3,0,2,1:T(8,128)(2,1)}, u32[]{:S(2)}) copy-start(bf16[256,1,1,128]{3,0,2,1:T(8,128)(2,1)} %copy-done.4) | copy-start | bytes 196612
  239.6 32.8 %copy-start.14 = (f32[2,128,16]{2,1,0:T(8,128)S(1)}, f32[2,128,16]{2,1,0:T(8,128)}, u32[]{:S(2)}) copy-start(f32[2,128,16]{2,1,0:T(8,128)} %get-tuple-element.30) | copy-start | bytes 49156
  239.6 34.2 %copy-start.55 = (f32[1,1,16]{2,1,0:T(1,128)S(1)}, f32[1,1,16]{2,1,0:T(1,128)}, u32[]{:S(2)}) copy-start(f32[1,1,16]{2,1,0:T(1,128)} %get-tuple-element.58) | copy-start | bytes 196
  239.6 140.7 %all-gather.20.cloned.1.call-start = ((), (), s32[]{:S(2)}) async-start(), calls=%async_computation.4 | async-start | bytes 4718592 | tf_op jit(solution)/shard_map/all_gather | solution.py:31
  329.8 50.5 %copy-start = (f32[2,16,8192]{2,1,0:T(8,128)S(1)}, f32[2,16,8192]{2,1,0:T(8,128)}, u32[]{:S(2)}) copy-start(f32[2,16,8192]{2,1,0:T(8,128)} %all-gather.16.cloned.1.call-done) | copy-start | bytes 3145732
  329.8 50.5 %copy-start.25 = (f32[16]{0:T(128)S(1)}, f32[16]{0:T(128)}, u32[]{:S(2)}) copy-start(f32[16]{0:T(128)} %copy-done.24) | copy-start | bytes 196
  329.8 50.5 %copy-start.27 = (f32[16]{0:T(128)S(1)}, f32[16]{0:T(128)}, u32[]{:S(2)}) copy-start(f32[16]{0:T(128)} %copy-done.26) | copy-start | bytes 196
  329.8 50.5 %copy-start.33 = (f32[16]{0:T(128)S(1)}, f32[16]{0:T(128)}, u32[]{:S(2)}) copy-start(f32[16]{0:T(128)} %copy-done.32) | copy-start | bytes 196
  329.9 50.5 %copy-start.39 = (f32[16]{0:T(128)S(1)}, f32[16]{0:T(128)}, u32[]{:S(2)}) copy-start(f32[16]{0:T(128)} %copy-done.38) | copy-start | bytes 196
  329.9 50.5 %copy-start.48 = (f32[16]{0:T(128)S(1)}, f32[16]{0:T(128)}, u32[]{:S(2)}) copy-start(f32[16]{0:T(128)} %get-tuple-element.75) | copy-start | bytes 196
  329.9 50.5 %copy-start.50 = (f32[16]{0:T(128)S(1)}, f32[16]{0:T(128)}, u32[]{:S(2)}) copy-start(f32[16]{0:T(128)} %get-tuple-element.18) | copy-start | bytes 196
  329.9 50.5 %copy-start.51 = (f32[16]{0:T(128)S(1)}, f32[16]{0:T(128)}, u32[]{:S(2)}) copy-start(f32[16]{0:T(128)} %get-tuple-element.19) | copy-start | bytes 196
  (44 other events, 685.8 us)
Sparse Core Ops, SparseCore 0:
  10.4 68.8 all-gather.13
  82.5 84.1 all-reduce.2
  172.3 18.1 all-gather.21
  192.9 15.3 all-gather.15
  210.5 26.7 all-gather.23
  239.6 27.3 all-gather.17
  268.7 55.7 all-gather.25
  326.9 53.3 all-gather.19
where the time goes:
time: 395 us
  waiting for transfers between devices  200 us (51%)
  blocking collectives  111 us (28%)
  other arithmetic  30.4 us (8%)
  local copies, waits for them, and re-layouts  26.2 us (7%)
  between operations  15 us (4%)
  matrix products  11.8 us (3%)
    all_gather x6, waiting for transfers between devices, prefix_by_axis(): pieces = jax.tree.map(lambda part: lax.all_gather(part, axis), so_far)  132 us
    psum x1, blocking collectives, body(): lax.psum((jnp.dot(owned, pieces[0], preferred_element_type=jnp.float32),...  67.7 us
    all_gather x1, waiting for transfers between devices, in_one_piece(): whole = lax.all_gather(both, axis, axis=dim, tiled=True)  54.7 us
    all_gather x6, blocking collectives, prefix_by_axis(): pieces = jax.tree.map(lambda part: lax.all_gather(part, axis), so_far)  42.9 us
    unnamed x134, local copies, waits for them, and re-layouts  15.8 us
    psum x1, waiting for transfers between devices, body(): lax.psum((jnp.dot(owned, pieces[0], preferred_element_type=jnp.float32),...  13.6 us
    add x6, other arithmetic, joined(): return (earlier[0] * later[0], later[0][:, None] * earlier[1] + later[1])  11 us
  transfers between devices with their start and end apart: 8, of which 7 were waited for; matrix products, arithmetic and copies ran while one was open for 13% of the time, Pallas kernels for 0%

commit v1 on v0

v1 whole, which is shorter than its diff:
```python
import functools

import jax
import jax.numpy as jnp
from jax import lax
from jax.experimental import pallas as pl
from jax.experimental.pallas import tpu as pltpu
from jax.sharding import Mesh
from jax.sharding import PartitionSpec as P

MESH = pl.DeviceIdType.MESH
SEQ = ("z", "xl", "c")
FSDP = ("xh", "y")
F32, BF16, I32 = jnp.float32, jnp.bfloat16, jnp.int32
NZ, NSLAB = 8, 32
SPAN, HEADS, WIDE = 128, 16, 1024
TOKENS = 256
VMEM = pl.BlockSpec(memory_space=pltpu.VMEM)
SMEM = pl.BlockSpec(memory_space=pltpu.SMEM)
ANY = pl.BlockSpec(memory_space=pl.ANY)


def iota(shape, dim):
    return lax.broadcasted_iota(I32, shape, dim)


def place():
    z, xl, c = lax.axis_index("z"), lax.axis_index("xl"), lax.axis_index("c")
    xh, y = lax.axis_index("xh"), lax.axis_index("y")
    return z, xl, c, xh, y


def dot(a, b, ca, cb):
    return lax.dot_general(a, b, (((ca,), (cb,)), ((), ())), preferred_element_type=F32)


def split3(v):
    hi = v.astype(BF16)
    rest = v - hi.astype(F32)
    mid = rest.astype(BF16)
    low = (rest - mid.astype(F32)).astype(BF16)
    return jnp.concatenate([hi, mid, low], axis=0)


def spread_matrix(shift):
    n = HEADS << shift
    same = (iota((48, n), 0) & 15) == (iota((48, n), 1) >> shift)
    return jnp.where(same, 1.0, 0.0).astype(BF16)


def per_head_column(row, scratch, first_head):
    scratch[...] = jnp.broadcast_to(row, (128, 128)).T
    return scratch[pl.ds(pl.multiple_of(first_head, HEADS), HEADS), :]


def segment_of(bounds, places):
    count = [jnp.where(places >= b, 1, 0).astype(I32) for b in bounds]
    return count[0] + count[1] + count[2]


def scalar_segment(bounds, position):
    count = [(position >= b).astype(I32) for b in bounds]
    return count[0] + count[1] + count[2]


def local_math(back, bvec, cvec, dt, rate, skip, x_ref, bounds, first, outs):
    pieces, decay, base, factor, inner, carry_row = outs
    wide = spread_matrix(6)
    tall = spread_matrix(7)
    rows, cols = iota((SPAN, SPAN), 0), iota((SPAN, SPAN), 1)
    upper = jnp.where(rows <= cols, 1.0, 0.0).astype(BF16)
    left_half = cols < 64
    sums, carries = [], []
    for blk in range(2):
        sl = slice(SPAN * blk, SPAN * blk + SPAN)
        b_blk, c_blk = bvec(blk), cvec(blk)
        dt_blk = dt[:, sl]
        parts = dot(split3(-(dt_blk * rate)), upper, 1, 0)
        cum = parts[0:16] + (parts[16:32] + parts[32:48])
        start = first + SPAN * blk
        mask = (segment_of(bounds, start + rows) == segment_of(bounds, start + cols)) & (rows >= cols)
        seg_end = scalar_segment(bounds, start + (SPAN - 1))
        seg_before = scalar_segment(bounds, start - 1)
        seg_row = segment_of(bounds, start + iota((HEADS, SPAN), 1))
        cum_end = jnp.broadcast_to(cum[:, SPAN - 1 : SPAN], (HEADS, SPAN))
        send = jnp.where(seg_row == seg_end, jnp.exp(cum_end - cum) * dt_blk, 0.0)
        read = jnp.where(seg_row == seg_before, jnp.exp(cum), 0.0)
        through = jnp.where(seg_end == seg_before, 1.0, 0.0)
        carry = jnp.exp(cum_end) * through
        both = dot(split3(jnp.where(iota((HEADS, SPAN), 1) < 64, carry, skip)), wide, 0, 0)
        carry_x, skip_x = both[0:8], both[64:65]
        scale_x = dot(split3(read if back else send), wide, 0, 0)
        factor[:, sl] = send if back else read
        sent = (x_ref[sl, :].astype(F32) * scale_x).astype(BF16)
        sums.append(dot(c_blk if back else b_blk, sent, 0, 0))
        carries.append(carry_x)
        scores = dot(c_blk, b_blk, 1, 1)
        column = dot(split3(cum), tall, 0, 0)
        for pair in range(8):
            lanes = slice(128 * pair, 128 * pair + 128)
            mixes = []
            for h in (2 * pair, 2 * pair + 1):
                gap = column[:, 128 * h : 128 * h + 128] - cum[h : h + 1, :]
                decays = jnp.exp(jnp.where(mask, gap, -1e30))
                mixes.append((decays * dt_blk[h : h + 1, :] * scores).astype(BF16))
            xp = x_ref[sl, lanes]
            zero = jnp.zeros_like(xp)
            x2 = jnp.concatenate([jnp.where(left_half, xp, zero), jnp.where(left_half, zero, xp)], axis=0)
            if back:
                inside = dot(jnp.concatenate(mixes, axis=0), x2, 0, 0)
            else:
                inside = dot(jnp.concatenate(mixes, axis=1), x2, 1, 0)
            base[sl, lanes] = inside + skip_x[:, lanes] * xp.astype(F32)
    early, late = (1, 0) if back else (0, 1)
    inner[...] = sums[early]
    carry_row[...] = carries[early]
    total = carries[late][0:1] * sums[early] + sums[late]
    both_decay = carries[0][0:1] * carries[1][0:1]
    for lg in range(4):
        decay[lg] = both_decay[:, 256 * lg : 256 * lg + 256]
        for ng in range(8):
            pieces[ng * 4 + lg] = total[16 * ng : 16 * ng + 16, 256 * lg : 256 * lg + 256].astype(BF16)


LOCAL_OUTS = (
    jax.ShapeDtypeStruct((NSLAB, 16, 256), BF16),
    jax.ShapeDtypeStruct((4, 1, 256), F32),
    jax.ShapeDtypeStruct((TOKENS, WIDE), F32),
    jax.ShapeDtypeStruct((HEADS, TOKENS), F32),
    jax.ShapeDtypeStruct((SPAN, WIDE), F32),
    jax.ShapeDtypeStruct((8, WIDE), F32),
)


def bounds_of(lengths):
    b1 = lengths[0]
    b2 = b1 + lengths[1]
    return (b1, b2, b2 + lengths[2])


def back_local_kernel(seg, bc_ref, dt_ref, g_ref, rate_ref, skip_ref, pdt_ref, *rest):
    outs, bvec_out, pdt_out = rest[:6], rest[6], rest[7]
    scratch, dt_pad = rest[8], rest[9]
    z, xl, c, xh, y = place()
    first = (z * 4 + xl * 2 + c) * TOKENS
    heads_first = (xh * 4 + y) * HEADS
    group = xh * 2 + y // 2
    lanes = iota((32, 128), 1)
    taps = pdt_ref[...].astype(F32)
    for g in range(4):
        turned = pltpu.roll(taps, lax.rem(32 * (y - g) + 128, 128), 1)
        mine = jnp.where((lanes >> 5) == y, turned, 0.0).astype(BF16)
        pdt_out[g, :, 0:128] = mine[0:16]
        pdt_out[g, :, 128:256] = mine[16:32]
    b_lanes = pl.ds(pl.multiple_of(group * 128, 128), 128)
    c_lanes = pl.ds(pl.multiple_of(group * 128 + 512, 128), 128)
    bvec_out[...] = bc_ref[:, b_lanes]
    dt_pad[...] = jnp.zeros_like(dt_pad)
    dt_pad[:, 0:HEADS] = dt_ref[...]
    dt = dt_pad[...].T[0:HEADS, :]
    rate = per_head_column(rate_ref[...], scratch, heads_first)
    skip = per_head_column(skip_ref[...], scratch, heads_first)
    local_math(
        True,
        lambda k: bc_ref[pl.ds(SPAN * k, SPAN), b_lanes],
        lambda k: bc_ref[pl.ds(SPAN * k, SPAN), c_lanes],
        dt, rate, skip, g_ref, bounds_of(seg), first, outs,
    )


def next_local_kernel(seg, bc_ref, dt_ref, x_ref, rate_ref, skip_ref, bias_ref, *rest):
    outs, scratch = rest[:6], rest[6]
    z, xl, c, xh, y = place()
    first = (z * 4 + xl * 2 + c) * TOKENS
    heads_first = (xh * 4 + y) * HEADS
    bias = per_head_column(bias_ref[...], scratch, heads_first)[:, 0:1]
    v = dt_ref[...] + bias
    dt = jnp.maximum(v, 0.0) + jnp.log1p(jnp.exp(-jnp.abs(v)))
    rate = per_head_column(rate_ref[...], scratch, heads_first)
    skip = per_head_column(skip_ref[...], scratch, heads_first)
    local_math(
        False,
        lambda k: bc_ref[pl.ds(SPAN * k, SPAN), 0:128],
        lambda k: bc_ref[pl.ds(SPAN * k, SPAN), 128:256],
        dt, rate, skip, x_ref, bounds_of(seg), first, outs,
    )


def final_math(back, pieces, base, factor, inner, carry_row, vec, out):
    first, second = (1, 0) if back else (0, 1)
    wide = spread_matrix(6)
    fl = slice(SPAN * first, SPAN * first + SPAN)
    sl = slice(SPAN * second, SPAN * second + SPAN)
    fac_f = dot(split3(factor[:, fl]), wide, 0, 0)
    fac_s = dot(split3(factor[:, sl]), wide, 0, 0)
    vec_f, vec_s = vec[fl, :], vec[sl, :]
    for lg in range(4):
        lanes = slice(256 * lg, 256 * lg + 256)
        state = jnp.concatenate([pieces[ng * 4 + lg] for ng in range(8)], axis=0)
        read_f = dot(vec_f, state, 1, 0)
        later = carry_row[0:1, lanes] * state.astype(F32) + inner[:, lanes]
        hi = later.astype(BF16)
        low = (later - hi.astype(F32)).astype(BF16)
        read_s = dot(vec_s, hi, 1, 0) + dot(vec_s, low, 1, 0)
        out[fl, lanes] = (base[fl, lanes] + fac_f[:, lanes] * read_f).astype(BF16)
        out[sl, lanes] = (base[sl, lanes] + fac_s[:, lanes] * read_s).astype(BF16)


def final_kernel(*refs):
    n_pieces, n_base, n_factor, n_inner, n_carry, bc = refs[:6]
    b_pieces, b_base, b_factor, b_inner, b_carry, bvec = refs[6:12]
    out_next, out_back = refs[12:14]
    final_math(False, n_pieces, n_base, n_factor, n_inner, n_carry, bc.at[:, 128:256], out_next)
    final_math(True, b_pieces, b_base, b_factor, b_inner, b_carry, bvec, out_back)


def slab_id(index):
    return {"z": index // 4, "xl": lax.rem(index // 2, 2), "c": lax.rem(index, 2)}


class Scan:
    def __init__(self, me, pieces, decay, inbox, decay_in, outbox, landed, sems):
        self.me, self.pieces, self.decay = me, pieces, decay
        self.inbox, self.decay_in, self.outbox, self.landed = inbox, decay_in, outbox, landed
        self.sems = sems

    def piece_copy(self, target, source):
        s, r = self.sems[0], self.sems[1]
        return pltpu.make_async_remote_copy(
            self.pieces.at[target], self.inbox.at[source], s.at[target], r.at[source],
            device_id=slab_id(target), device_id_type=MESH)

    def decay_copy(self, target, source):
        s, r = self.sems[2], self.sems[3]
        return pltpu.make_async_remote_copy(
            self.decay.at[lax.rem(target, 4)], self.decay_in.at[source], s.at[target], r.at[source],
            device_id=slab_id(target), device_id_type=MESH)

    def state_copy(self, target, source):
        s, r = self.sems[4], self.sems[5]
        return pltpu.make_async_remote_copy(
            self.outbox.at[target], self.landed.at[source], s.at[target], r.at[source],
            device_id=slab_id(target), device_id_type=MESH)

    def others(self, body):
        def step(d, carry):
            body(lax.rem(self.me + d, NSLAB))
            return carry

        lax.fori_loop(1, NSLAB, step, 0)

    def send_pieces(self):
        def go(j):
            self.piece_copy(j, self.me).start()
            self.decay_copy(j, self.me).start()

        self.others(go)
        self.inbox[self.me] = self.pieces[self.me]
        self.decay_in[self.me] = self.decay[lax.rem(self.me, 4)]

    def prefix(self, back):
        def arrive(j):
            self.piece_copy(j, j).wait_recv()
            self.decay_copy(j, j).wait_recv()

        self.others(arrive)

        def step(k, state):
            j = NSLAB - 1 - k if back else k
            self.outbox[j] = state.astype(BF16)
            return self.decay_in[j] * state + self.inbox[j].astype(F32)

        lax.fori_loop(0, NSLAB, step, jnp.zeros((16, 256), F32))

    def send_states(self):
        self.others(lambda j: self.state_copy(j, self.me).start())
        self.landed[self.me] = self.outbox[self.me]

    def finish(self):
        def done(j):
            self.state_copy(j, j).wait_recv()
            self.piece_copy(j, self.me).wait_send()
            self.decay_copy(j, self.me).wait_send()
            self.state_copy(j, self.me).wait_send()

        self.others(done)


SCAN_SCRATCH = [
    pltpu.VMEM((NSLAB, 16, 256), BF16),
    pltpu.VMEM((NSLAB, 1, 256), F32),
    pltpu.VMEM((NSLAB, 16, 256), BF16),
    pltpu.VMEM((NSLAB, 16, 256), BF16),
] + [pltpu.SemaphoreType.DMA((NSLAB,))] * 6


def next_scan_kernel(pieces, decay, out, inbox, decay_in, outbox, landed, *sems):
    z, xl, c, xh, y = place()
    me = z * 4 + xl * 2 + c
    scan = Scan(me, pieces, decay, inbox, decay_in, outbox, landed, sems)
    barrier = pltpu.get_barrier_semaphore()
    scan.others(lambda j: pl.semaphore_signal(barrier, inc=1, device_id=slab_id(j), device_id_type=MESH))
    pl.semaphore_wait(barrier, NSLAB - 1)
    scan.send_pieces()
    scan.prefix(False)
    scan.send_states()
    scan.finish()
    out[...] = landed[...]


def project_kernel(hid, pbc, pdt, pieces, decay, bc_out, dt_out, state_out,
                   wbuf, ptmp, hbuf, acc, dts, bc_send, bc_recv, dt_recv,
                   hid_sem, a2a_send, a2a_recv, ring_send, ring_recv, pair_send, pair_recv,
                   inbox, decay_in, outbox, landed, *sems):
    z, xl, c, xh, y = place()
    me = z * 4 + xl * 2 + c
    half = lax.rem(y, 2)
    y_pair = y + 1 - 2 * half
    scan = Scan(me, pieces, decay, inbox, decay_in, outbox, landed, sems)

    barrier = pltpu.get_barrier_semaphore()

    def greet(**where):
        pl.semaphore_signal(barrier, inc=1, device_id=where, device_id_type=MESH)

    scan.others(lambda j: greet(**slab_id(j)))
    greet(y=y_pair)
    own_in_group = xh == half
    for src in range(4):
        @pl.when(jnp.logical_not(own_in_group & (y == src)))
        def _():
            greet(xh=half, y=jnp.int32(src))

    hid_copies = []
    for j in range(NSLAB):
        lanes = pl.ds(pl.multiple_of(256 * j + 128 * half, 128), 128)
        copy = pltpu.make_async_copy(hid.at[:, lanes], hbuf.at[:, pl.ds(128 * j, 128)], hid_sem.at[j])
        copy.start()
        hid_copies.append(copy)

    @pl.when(own_in_group)
    def _():
        pl.semaphore_wait(barrier, NSLAB - 1 + 1 + 3)

    @pl.when(jnp.logical_not(own_in_group))
    def _():
        pl.semaphore_wait(barrier, NSLAB - 1 + 1 + 4)

    my_rows = pl.ds(pl.multiple_of(32 * y, 32), 32)

    def spread_copies(g, source, where):
        rows = pl.ds(pl.multiple_of(32 * source, 32), 32)
        return [
            pltpu.make_async_remote_copy(
                pbc.at[:, pl.ds(128 * g, 128)], wbuf.at[me, rows, pl.ds(0, 128)],
                a2a_send.at[g, 0], a2a_recv.at[source, 0], device_id=where, device_id_type=MESH),
            pltpu.make_async_remote_copy(
                pbc.at[:, pl.ds(512 + 128 * g, 128)], wbuf.at[me, rows, pl.ds(128, 128)],
                a2a_send.at[g, 1], a2a_recv.at[source, 1], device_id=where, device_id_type=MESH),
            pltpu.make_async_remote_copy(
                pdt.at[g], ptmp.at[source],
                a2a_send.at[g, 2], a2a_recv.at[source, 2], device_id=where, device_id_type=MESH),
        ]

    for g in range(4):
        to_y = 2 * (g % 2) + xh
        mine = (xh == g // 2) & (y == to_y)
        where = {"xh": jnp.int32(g // 2), "y": to_y}

        @pl.when(jnp.logical_not(mine))
        def _():
            for copy in spread_copies(g, y, where):
                copy.start()

        @pl.when(mine)
        def _():
            wbuf[me, my_rows, 0:128] = pbc[:, 128 * g : 128 * g + 128]
            wbuf[me, my_rows, 128:256] = pbc[:, 512 + 128 * g : 512 + 128 * g + 128]
            ptmp[y] = pdt[g]

    scan.send_pieces()

    for src in range(4):
        @pl.when(jnp.logical_not(own_in_group & (y == src)))
        def _():
            for copy in spread_copies(0, src, {"xh": half, "y": jnp.int32(src)}):
                copy.wait_recv()

    packed = (ptmp[0].astype(F32) + ptmp[1].astype(F32)) + (ptmp[2].astype(F32) + ptmp[3].astype(F32))
    wbuf[me, 128:144, :] = packed.astype(BF16)

    right, left = lax.rem(z + 1, NZ), lax.rem(z + NZ - 1, NZ)
    ROWS = (pl.ds(0, 64), pl.ds(64, 80))
    sends = []

    def forward(slot, chunk, **where):
        part = wbuf.at[slot, ROWS[chunk]]
        copy = pltpu.make_async_remote_copy(
            part, part, ring_send.at[len(sends)], ring_recv.at[slot, chunk],
            device_id=where, device_id_type=MESH)
        copy.start()
        sends.append(copy)

    def arrive(slot, chunk):
        part = wbuf.at[slot, ROWS[chunk]]
        pltpu.make_async_remote_copy(
            part, part, ring_send.at[0], ring_recv.at[slot, chunk],
            device_id={"z": right}, device_id_type=MESH).wait_recv()

    mate = me + 2 - 4 * xl
    sibling = me + 1 - 2 * c
    other_x, other_c = 1 - xl, 1 - c
    for chunk in (0, 1):
        forward(me, chunk, xl=other_x)
        forward(me, chunk, z=right)
        forward(me, chunk, z=left)
    for chunk in (0, 1):
        forward(me, chunk, c=other_c)
    arrive(mate, 0)
    forward(mate, 0, z=right)
    forward(mate, 0, z=left)
    forward(mate, 0, c=other_c)
    last = {0: (1,), 1: (0, 2)}
    late = [mate]
    for hop in range(1, 5):
        fresh = []
        for chunk in (0, 1, 2):
            for side in (0, 1):
                if hop == 4 and chunk not in last[side]:
                    continue
                oz = lax.rem(z + NZ - hop, NZ) if side == 0 else lax.rem(z + hop, NZ)
                column = oz * 4 + xl * 2 + c
                across = oz * 4 + other_x * 2 + c
                slot, part = (across, 0) if chunk == 2 else (column, chunk)
                arrive(slot, part)
                if hop < 3 or (hop == 3 and chunk in last[side]):
                    forward(slot, part, z=right if side == 0 else left)
                if chunk == 1:
                    forward(slot, 1, xl=other_x)
                    fresh.append(across)
                forward(slot, part, c=other_c)
        for slot in late:
            arrive(slot, 1)
            forward(slot, 1, c=other_c)
        late = fresh
    for slot in late:
        arrive(slot, 1)
        forward(slot, 1, c=other_c)

    scan.prefix(True)
    scan.send_states()

    for copy in hid_copies:
        copy.wait()
    for oz in range(NZ):
        for ox in range(2):
            for chunk in (0, 1):
                arrive(oz * 4 + ox * 2 + other_c, chunk)

    acc[...] = jnp.zeros_like(acc)
    lane_class = iota((32, 128), 1) >> 5

    def multiply(j, carry):
        columns = hbuf[:, pl.ds(pl.multiple_of(256 * j, 256), 256)]
        weights, taps = [], []
        for k in (2 * j, 2 * j + 1):
            weights.append(wbuf[k, 0:128, :])
            low = wbuf[k, 128:144, :].astype(F32)
            block = jnp.concatenate([low[:, 0:128], low[:, 128:256]], axis=0)
            taps += [jnp.where(lane_class == i, block, 0.0) for i in range(4)]
        acc[:, 0:256] += dot(columns, jnp.concatenate(weights, axis=0), 1, 0)
        acc[:, 256:384] += dot(columns, jnp.concatenate(taps, axis=0).astype(BF16), 1, 0)
        return carry

    lax.fori_loop(0, 16, multiply, 0)

    folded = acc[:, 256:384].T
    dts[...] = (folded[0:32] + folded[32:64]) + (folded[64:96] + folded[96:128])
    bc_send[...] = acc[:, 0:256].astype(BF16)
    pair = [
        pltpu.make_async_remote_copy(
            bc_send, bc_recv, pair_send.at[0], pair_recv.at[0],
            device_id={"y": y_pair}, device_id_type=MESH),
        pltpu.make_async_remote_copy(
            dts.at[pl.ds(pl.multiple_of(16 - 16 * half, 16), 16)], dt_recv, pair_send.at[1], pair_recv.at[1],
            device_id={"y": y_pair}, device_id_type=MESH),
    ]
    for copy in pair:
        copy.start()
    for copy in pair:
        copy.wait_recv()
    bc_out[...] = (acc[:, 0:256] + bc_recv[...].astype(F32)).astype(BF16)
    dt_out[...] = dts[pl.ds(pl.multiple_of(16 * half, 16), 16)] + dt_recv[...]

    for g in range(4):
        to_y = 2 * (g % 2) + xh
        mine = (xh == g // 2) & (y == to_y)

        @pl.when(jnp.logical_not(mine))
        def _():
            for copy in spread_copies(g, y, {"xh": jnp.int32(g // 2), "y": to_y}):
                copy.wait_send()

    for copy in sends:
        copy.wait_send()
    for copy in pair:
        copy.wait_send()
    scan.finish()
    state_out[...] = landed[...]


def params(limit_mib, **kw):
    return pltpu.CompilerParams(vmem_limit_bytes=limit_mib << 20, **kw)


def body(hidden_next, values_next, seg_next, proj_bc, proj_dt, dt_bias, decay_rate, skip_gain,
         bc_prev, dt_prev, seg_prev, grad_prev):
    as_row = lambda a: a.reshape(1, 128)
    bias, rate, skip = as_row(dt_bias), as_row(decay_rate), as_row(skip_gain)
    sds = jax.ShapeDtypeStruct
    *back, bvec, pdt = pl.pallas_call(
        back_local_kernel,
        out_shape=LOCAL_OUTS + (sds((TOKENS, 128), BF16), sds((4, 16, 256), BF16)),
        in_specs=[SMEM] + [VMEM] * 6,
        out_specs=(VMEM,) * 8,
        scratch_shapes=[pltpu.VMEM((128, 128), F32), pltpu.VMEM((TOKENS, 128), F32)],
        compiler_params=params(40),
        name="back_local",
    )(seg_prev, bc_prev, dt_prev, grad_prev, rate, skip, proj_dt)
    bc, dt_pre, back_states = pl.pallas_call(
        project_kernel,
        out_shape=(sds((TOKENS, 256), BF16), sds((HEADS, TOKENS), F32), sds((NSLAB, 16, 256), BF16)),
        in_specs=[ANY] + [VMEM] * 4,
        out_specs=(VMEM,) * 3,
        scratch_shapes=[
            pltpu.VMEM((NSLAB, 144, 256), BF16),
            pltpu.VMEM((4, 16, 256), BF16),
            pltpu.VMEM((TOKENS, 4096), BF16),
            pltpu.VMEM((TOKENS, 384), F32),
            pltpu.VMEM((32, TOKENS), F32),
            pltpu.VMEM((TOKENS, 256), BF16),
            pltpu.VMEM((TOKENS, 256), BF16),
            pltpu.VMEM((HEADS, TOKENS), F32),
            pltpu.SemaphoreType.DMA((NSLAB,)),
            pltpu.SemaphoreType.DMA((4, 3)),
            pltpu.SemaphoreType.DMA((4, 3)),
            pltpu.SemaphoreType.DMA((80,)),
            pltpu.SemaphoreType.DMA((NSLAB, 2)),
            pltpu.SemaphoreType.DMA((2,)),
            pltpu.SemaphoreType.DMA((2,)),
        ] + SCAN_SCRATCH,
        compiler_params=params(40, collective_id=0, has_side_effects=True),
        name="project",
    )(hidden_next, proj_bc, pdt, back[0], back[1])
    nxt = pl.pallas_call(
        next_local_kernel,
        out_shape=LOCAL_OUTS,
        in_specs=[SMEM] + [VMEM] * 6,
        out_specs=(VMEM,) * 6,
        scratch_shapes=[pltpu.VMEM((128, 128), F32)],
        compiler_params=params(40),
        name="next_local",
    )(seg_next, bc, dt_pre, values_next, rate, skip, bias)
    next_states = pl.pallas_call(
        next_scan_kernel,
        out_shape=sds((NSLAB, 16, 256), BF16),
        in_specs=[VMEM] * 2,
        out_specs=VMEM,
        scratch_shapes=SCAN_SCRATCH,
        compiler_params=params(16, collective_id=1, has_side_effects=True),
        name="next_scan",
    )(nxt[0], nxt[1])
    return pl.pallas_call(
        final_kernel,
        out_shape=(sds((TOKENS, WIDE), BF16), sds((TOKENS, WIDE), BF16)),
        in_specs=[VMEM] * 12,
        out_specs=(VMEM,) * 2,
        compiler_params=params(40),
        name="final",
    )(next_states, *nxt[2:], bc, back_states, *back[2:], bvec)


def solution(mesh):
    split = Mesh(mesh.devices.reshape(8, 2, 2, 2, 4), ("z", "xl", "c", "xh", "y"))
    tokens, both, rows = P(SEQ, None), P(SEQ, FSDP), P(SEQ + FSDP, None)
    in_specs = (tokens, both, P(), rows, rows, P(), P(), P(), tokens, both, P(), both)
    return jax.shard_map(body, mesh=split, in_specs=in_specs, out_specs=(both, both), check_vma=False)
```

time: 395 us -> 90.8 us (0.23)
  waiting for transfers between devices: 200 us -> 0 us
  blocking collectives: 111 us -> 0 us
  Pallas kernels: 0 us -> 81 us
  other arithmetic: 30.4 us -> 0 us
  local copies, waits for them, and re-layouts: 26.2 us -> 8.62 us
  between operations: 15 us -> 0.75 us
  matrix products: 11.8 us -> 0 us
    all_gather x7 -> x0, waiting for transfers between devices: 187 us -> none  [the longest x6 132 us: prefix_by_axis(): pieces = jax.tree.map(lambda part: lax.all_gather(part, axis), so_far)]
    pallas_call x0 -> x5, Pallas kernels: none -> 81 us  [the longest x1 46.5 us: body(): pl.pallas_call(project_kernel, out_shape=(sds((TOKENS, 256), BF16), sds((...]
    psum x1 -> x0, blocking collectives: 67.7 us -> none  [body(): lax.psum((jnp.dot(owned, pieces[0], preferred_element_type=jnp.float32),...]
    all_gather x6 -> x0, blocking collectives: 42.9 us -> none  [prefix_by_axis(): pieces = jax.tree.map(lambda part: lax.all_gather(part, axis), so_far)]
    psum x1 -> x0, waiting for transfers between devices: 13.6 us -> none  [body(): lax.psum((jnp.dot(owned, pieces[0], preferred_element_type=jnp.float32),...]
    dot_general x10 -> x0, matrix products: 11.8 us -> none  [the longest x1 2.7 us: body(): jnp.einsum('khts,kshp->kthp', mixing, inputs, preferred_element_type=jnp....]
    add x6 -> x0, other arithmetic: 11 us -> none  [joined(): return (earlier[0] * later[0], later[0][:, None] * earlier[1] + later[1])]
    unnamed x4 -> x0, other arithmetic: 7.55 us -> none
  transfers between devices with their start and end apart: 8 -> 0, of which waited for: 7 -> 0; matrix products, arithmetic and copies ran while one was open for 13% -> 0% of each run, Pallas kernels for 0% -> 0%
where the time goes in v1:
time: 90.8 us; the launch traced here: 90.4 us
  Pallas kernels  81 us (89%)
  local copies, waits for them, and re-layouts  8.62 us (9%)
    pallas_call x1, Pallas kernels, body(): pl.pallas_call(project_kernel, out_shape=(sds((TOKENS, 256), BF16), sds((...  46.5 us
    pallas_call x1, Pallas kernels, body(): pl.pallas_call(next_scan_kernel, out_shape=sds((NSLAB, 16, 256), BF16), i...  26.8 us
    unnamed x27, local copies, waits for them, and re-layouts  8.62 us
    pallas_call x1, Pallas kernels, body(): pl.pallas_call(next_local_kernel, out_shape=LOCAL_OUTS, in_specs=[SMEM] +...  2.99 us
    pallas_call x1, Pallas kernels, body(): pl.pallas_call(back_local_kernel, out_shape=LOCAL_OUTS + (sds((TOKENS, 12...  2.91 us

profile of v1, /device:TPU:1, one launch (start us, length us, event | category | flops | bytes accessed | tf_op | source)
XLA Modules:
  0.0 90.4 jit_solution(7070210477787152690)
XLA Ops:
  0.6 0.0 copy-start.9
  0.6 0.0 copy-start.7
  0.7 0.0 copy-start.12
  0.7 0.0 copy-start.11
  0.7 0.8 copy.14.dt_ref
  1.5 1.0 %copy-done.1 = bf16[256,1024]{1,0:T(8,128)(2,1)S(1)} copy-done((bf16[256,1024]{1,0:T(8,128)(2,1)S(1)}, bf16[256,1024]{1,0:T(8,128)(2,1)}, u32[]{:S(2)}) %copy-start.1) | copy-done | bytes 524312
  2.6 1.0 %copy-done.2 = bf16[256,1024]{1,0:T(8,128)(2,1)S(1)} copy-done((bf16[256,1024]{1,0:T(8,128)(2,1)S(1)}, bf16[256,1024]{1,0:T(8,128)(2,1)}, u32[]{:S(2)}) %copy-start.2) | copy-done | bytes 524312
  3.6 0.7 copy-done.5
  4.3 0.7 copy-done.6
  5.0 0.7 copy-done.8
  5.6 0.7 copy-done.10
  6.3 2.9 %back_local.1 = (bf16[32,16,256]{2,1,0:T(8,128)(2,1)S(1)}, f32[4,1,256]{2,1,0:T(1,128)S(1)}, f32[256,1024]{1,0:T(8,128)S(1)}, f32[16,256]{1,0:T(8,128)S(1)}, f32...) custom-call(s32[4]{0:T(128)S(1)} %copy-done.10, ...), custom_call_target="tpu_custom_call" | custom-call | tf_op jit(solution)/shard_map/back_local/pallas_call | solution.py:521
  9.2 0.0 copy-start
  9.2 2.2 %copy-done = bf16[256,8192]{1,0:T(8,128)(2,1)S(1)} copy-done((bf16[256,8192]{1,0:T(8,128)(2,1)S(1)}, bf16[256,8192]{1,0:T(8,128)(2,1)}, u32[]{:S(2)}) %copy-start) | copy-done | bytes 4194328
  11.4 0.8 copy-done.4
  12.2 46.5 %project.1 = (bf16[256,256]{1,0:T(8,128)(2,1)S(1)}, f32[16,256]{1,0:T(8,128)S(1)}, bf16[32,16,256]{2,1,0:T(8,128)(2,1)S(1)}) custom-call(bf16[256,8192]{1,0:T(8,128)(2,1)S(1)} %copy-done, bf16[32,1024]{1,0:T(8,128)(2,1)S(1)} %copy-done.4, bf16[4,16,256]{2,1,0:T(8,128)(2,1)S(1)} %get-tuple-element.19.pdt, bf16[32,16,256]{2,1,0:T(8,128)(2,1)S(1)} %get-tuple-element.20.pieces, ...), custom_call_target="tpu_custom_call" | custom-call | tf_op jit(solution)/shard_map/project/pallas_call | solution.py:530
  58.7 0.0 copy-done.9
  58.7 0.0 copy-done.7
  58.8 0.0 copy-done.12
  58.8 0.0 copy-done.11
  58.8 0.0 copy-done.3
  58.8 3.0 %next_local.1 = (bf16[32,16,256]{2,1,0:T(8,128)(2,1)S(1)}, f32[4,1,256]{2,1,0:T(1,128)S(1)}, f32[256,1024]{1,0:T(8,128)S(1)}, f32[16,256]{1,0:T(8,128)S(1)}, f32...) custom-call(s32[4]{0:T(128)S(1)} %copy-done.11, bf16[256,256]{1,0:T(8,128)(2,1)S(1)} %get-tuple-element.22.bc_ref.refs_5_, ...), custom_call_target="tpu_custom_call" | custom-call | tf_op jit(solution)/shard_map/next_local/pallas_call | solution.py:555
  61.8 26.8 %next_scan.1.refs_0_ = bf16[32,16,256]{2,1,0:T(8,128)(2,1)S(1)} custom-call(bf16[32,16,256]{2,1,0:T(8,128)(2,1)S(1)} %get-tuple-element.24.pieces, f32[4,1,256]{2,1,0:T(1,128)S(1)} %get-tuple-element.25.decay), custom_call_target="tpu_custom_call" | custom-call | tf_op jit(solution)/shard_map/next_scan/pallas_call | solution.py:564
  88.6 1.8 %final.1 = (bf16[256,1024]{1,0:T(8,128)(2,1)}, bf16[256,1024]{1,0:T(8,128)(2,1)}) custom-call(bf16[32,16,256]{2,1,0:T(8,128)(2,1)S(1)} %next_scan.1.refs_0_, f32[256,1024]{1,0:T(8,128)S(1)} %get-tuple-element.26.refs_1_, f32[16,256]{1,0:T(8,128)S(1)} %get-tuple-element.27.refs_2_, f32[128,1024]{1,0:T(8,128)S(1)} %get-tuple-element.28.refs_3_, ...), custom_call_target="tpu_custom_call" | custom-call | tf_op jit(solution)/shard_map/final/pallas_call | solution.py:573
  (8 shorter events, 0.0 us)
Async XLA Ops:
  0.6 58.1 %copy-start.9 = (f32[128]{0:T(128)S(1)}, f32[128]{0:T(128)}, u32[]{:S(2)}) copy-start(f32[128]{0:T(128)} %param.19) | copy-start | bytes 1540
  0.6 58.1 %copy-start.7 = (f32[128]{0:T(128)S(1)}, f32[128]{0:T(128)}, u32[]{:S(2)}) copy-start(f32[128]{0:T(128)} %param.18) | copy-start | bytes 1540
  0.7 58.1 %copy-start.12 = (f32[128]{0:T(128)S(1)}, f32[128]{0:T(128)}, u32[]{:S(2)}) copy-start(f32[128]{0:T(128)} %param.17) | copy-start | bytes 1540
  0.7 58.1 %copy-start.11 = (s32[4]{0:T(128)S(1)}, s32[4]{0:T(128)}, u32[]{:S(2)}) copy-start(s32[4]{0:T(128)} %seg.3) | copy-start | bytes 52
  1.5 1.0 %copy-start.1 = (bf16[256,1024]{1,0:T(8,128)(2,1)S(1)}, bf16[256,1024]{1,0:T(8,128)(2,1)}, u32[]{:S(2)}) copy-start(bf16[256,1024]{1,0:T(8,128)(2,1)} %bc_ref.1) | copy-start | bytes 1572868
  2.6 1.0 %copy-start.2 = (bf16[256,1024]{1,0:T(8,128)(2,1)S(1)}, bf16[256,1024]{1,0:T(8,128)(2,1)}, u32[]{:S(2)}) copy-start(bf16[256,1024]{1,0:T(8,128)(2,1)} %g_ref.1) | copy-start | bytes 1572868
  3.6 0.7 copy-start.5
  4.3 0.7 copy-start.6
  5.0 0.7 copy-start.8
  5.6 0.7 copy-start.10
  6.3 52.5 %copy-start.3 = (bf16[256,1024]{1,0:T(8,128)(2,1)S(1)}, bf16[256,1024]{1,0:T(8,128)(2,1)}, u32[]{:S(2)}) copy-start(bf16[256,1024]{1,0:T(8,128)(2,1)} %x_ref.1) | copy-start | bytes 1572868
  9.2 2.2 %copy-start = (bf16[256,8192]{1,0:T(8,128)(2,1)S(1)}, bf16[256,8192]{1,0:T(8,128)(2,1)}, u32[]{:S(2)}) copy-start(bf16[256,8192]{1,0:T(8,128)(2,1)} %hid.1) | copy-start | bytes 12582916
  11.4 0.8 copy-start.4

commit v2 on v1

v2 whole, which is shorter than its diff:
```python
import functools

import jax
import jax.numpy as jnp
from jax import lax
from jax.experimental import pallas as pl
from jax.experimental.pallas import tpu as pltpu
from jax.sharding import Mesh
from jax.sharding import PartitionSpec as P

MESH = pl.DeviceIdType.MESH
SEQ = ("z", "xl", "c")
FSDP = ("xh", "y")
F32, BF16, I32 = jnp.float32, jnp.bfloat16, jnp.int32
NZ, NSLAB = 8, 32
SPAN, HEADS, WIDE = 128, 16, 1024
TOKENS = 256
VMEM = pl.BlockSpec(memory_space=pltpu.VMEM)
SMEM = pl.BlockSpec(memory_space=pltpu.SMEM)
ANY = pl.BlockSpec(memory_space=pl.ANY)


def iota(shape, dim):
    return lax.broadcasted_iota(I32, shape, dim)


def place():
    z, xl, c = lax.axis_index("z"), lax.axis_index("xl"), lax.axis_index("c")
    xh, y = lax.axis_index("xh"), lax.axis_index("y")
    return z, xl, c, xh, y


def dot(a, b, ca, cb):
    return lax.dot_general(a, b, (((ca,), (cb,)), ((), ())), preferred_element_type=F32)


def split3(v):
    hi = v.astype(BF16)
    rest = v - hi.astype(F32)
    mid = rest.astype(BF16)
    low = (rest - mid.astype(F32)).astype(BF16)
    return jnp.concatenate([hi, mid, low], axis=0)


def spread_matrix(shift):
    n = HEADS << shift
    same = (iota((48, n), 0) & 15) == (iota((48, n), 1) >> shift)
    return jnp.where(same, 1.0, 0.0).astype(BF16)


def per_head_column(row, scratch, first_head):
    scratch[...] = jnp.broadcast_to(row, (128, 128)).T
    return scratch[pl.ds(pl.multiple_of(first_head, HEADS), HEADS), :]


def segment_of(bounds, places):
    count = [jnp.where(places >= b, 1, 0).astype(I32) for b in bounds]
    return count[0] + count[1] + count[2]


def scalar_segment(bounds, position):
    count = [(position >= b).astype(I32) for b in bounds]
    return count[0] + count[1] + count[2]


def bounds_of(lengths):
    b1 = lengths[0]
    b2 = b1 + lengths[1]
    return (b1, b2, b2 + lengths[2])


class Side:
    def __init__(self, back, refs, first, bounds, rate, skip):
        (self.bv, self.cv, self.values, self.dt, self.cum, self.factor, self.base, self.inner, self.carry_row,
         self.total, self.decay) = refs
        self.back, self.first, self.bounds, self.rate, self.skip = back, first, bounds, rate, skip

    def summarize(self):
        wide = spread_matrix(6)
        rows, cols = iota((SPAN, SPAN), 0), iota((SPAN, SPAN), 1)
        upper = jnp.where(rows <= cols, 1.0, 0.0).astype(BF16)
        back, bounds = self.back, self.bounds
        sums, carries = [], []
        for blk in range(2):
            sl = slice(SPAN * blk, SPAN * blk + SPAN)
            dt = self.dt[:, sl]
            parts = dot(split3(-(dt * self.rate[...])), upper, 1, 0)
            cum = parts[0:16] + (parts[16:32] + parts[32:48])
            self.cum[:, sl] = cum
            start = self.first + SPAN * blk
            seg_end = scalar_segment(bounds, start + (SPAN - 1))
            seg_before = scalar_segment(bounds, start - 1)
            seg_row = segment_of(bounds, start + iota((HEADS, SPAN), 1))
            cum_end = jnp.broadcast_to(cum[:, SPAN - 1 : SPAN], (HEADS, SPAN))
            send = jnp.where(seg_row == seg_end, jnp.exp(cum_end - cum) * dt, 0.0)
            read = jnp.where(seg_row == seg_before, jnp.exp(cum), 0.0)
            carry = jnp.exp(cum_end) * jnp.where(seg_end == seg_before, 1.0, 0.0)
            carries.append(dot(split3(carry), wide, 0, 0)[0:8])
            self.factor[:, sl] = send if back else read
            scale = dot(split3(read if back else send), wide, 0, 0)
            sent = (self.values[sl, :].astype(F32) * scale).astype(BF16)
            sums.append(dot((self.cv if back else self.bv)[sl, :], sent, 0, 0))
        early, late = (1, 0) if back else (0, 1)
        self.inner[...] = sums[early]
        self.carry_row[...] = carries[early]
        self.total[...] = carries[late][0:1] * sums[early] + sums[late]
        self.decay[...] = carries[0] * carries[1]

    def within(self):
        tall = spread_matrix(7)
        wide = spread_matrix(6)
        rows, cols = iota((SPAN, SPAN), 0), iota((SPAN, SPAN), 1)
        left_half = cols < 64
        back, bounds = self.back, self.bounds
        skip_x = dot(split3(self.skip[...]), wide, 0, 0)[0:1]

        def block(blk, carry):
            sl = pl.ds(pl.multiple_of(SPAN * blk, SPAN), SPAN)
            cum, dt = self.cum[:, sl], self.dt[:, sl]
            start = self.first + SPAN * blk
            mask = (segment_of(bounds, start + rows) == segment_of(bounds, start + cols)) & (rows >= cols)
            scores = dot(self.cv[sl, :], self.bv[sl, :], 1, 1)
            column = dot(split3(cum), tall, 0, 0)
            for pair in range(8):
                lanes = slice(128 * pair, 128 * pair + 128)
                mixes = []
                for h in (2 * pair, 2 * pair + 1):
                    gap = column[:, 128 * h : 128 * h + 128] - cum[h : h + 1, :]
                    decays = jnp.exp(jnp.where(mask, gap, -1e30))
                    mixes.append((decays * dt[h : h + 1, :] * scores).astype(BF16))
                xp = self.values[sl, lanes]
                zero = jnp.zeros_like(xp)
                x2 = jnp.concatenate([jnp.where(left_half, xp, zero), jnp.where(left_half, zero, xp)], axis=0)
                if back:
                    inside = dot(jnp.concatenate(mixes, axis=0), x2, 0, 0)
                else:
                    inside = dot(jnp.concatenate(mixes, axis=1), x2, 1, 0)
                self.base[sl, lanes] = inside + skip_x[:, lanes] * xp.astype(F32)
            return carry

        lax.fori_loop(0, 2, block, 0)

    def finish(self, state, out):
        wide = spread_matrix(6)
        first, second = (1, 0) if self.back else (0, 1)
        vec = self.bv if self.back else self.cv
        for blk, later in ((first, False), (second, True)):
            sl = slice(SPAN * blk, SPAN * blk + SPAN)
            scale = dot(split3(self.factor[:, sl]), wide, 0, 0)
            for half in range(2):
                lanes = slice(512 * half, 512 * half + 512)
                now = state[half]
                if later:
                    now = self.carry_row[0:1, lanes] * now + self.inner[:, lanes]
                hi = now.astype(BF16)
                low = (now - hi.astype(F32)).astype(BF16)
                read = dot(vec[sl, :], hi, 1, 0) + dot(vec[sl, :], low, 1, 0)
                out[sl, lanes] = (self.base[sl, lanes] + scale[:, lanes] * read).astype(BF16)


NCHIP = 16


def chip_id(q):
    return {"z": q // 2, "xl": lax.rem(q, 2)}


class Scan:
    def __init__(self, back, me, core, total, decay, refs):
        self.back, self.me, self.core, self.total, self.decay = back, me, core, total, decay
        (self.sib_total, self.sib_decay, self.pieces, self.steps, self.inbox, self.decay_in, self.outbox, self.landed,
         self.away, self.state) = refs[:10]
        self.sems = refs[10:]

    def to_chip(self, src, dst, k, target, source):
        return pltpu.make_async_remote_copy(
            src, dst, self.sems[k].at[target], self.sems[k + 1].at[source],
            device_id=chip_id(target), device_id_type=MESH)

    def piece_copy(self, target, source):
        return self.to_chip(self.pieces.at[target], self.inbox.at[source], 0, target, source)

    def decay_copy(self, target, source):
        return self.to_chip(self.steps.at[lax.rem(target, 2)], self.decay_in.at[source], 2, target, source)

    def state_copy(self, target, source):
        return self.to_chip(self.outbox.at[target], self.landed.at[source], 4, target, source)

    def to_sibling(self, src, dst, k):
        return pltpu.make_async_remote_copy(
            src, dst, self.sems[6].at[k], self.sems[7].at[k],
            device_id={"c": 1 - self.core}, device_id_type=MESH)

    def lanes(self, core):
        return pl.ds(pl.multiple_of(512 * core, 512), 512)

    def sibling_copies(self):
        theirs = self.lanes(1 - self.core)
        return (self.to_sibling(self.total.at[:, theirs], self.sib_total, 0),
                self.to_sibling(self.decay.at[:, theirs], self.sib_decay, 1))

    def back_copy(self):
        return self.to_sibling(self.away, self.state.at[self.core], 2)

    def others(self, body):
        def step(d, carry):
            body(lax.rem(self.me + d, NCHIP))
            return carry

        lax.fori_loop(1, NCHIP, step, 0)

    def share(self):
        for copy in self.sibling_copies():
            copy.start()

    def two_slabs(self):
        mine = self.lanes(self.core)
        own, own_decay = self.total[:, mine], self.decay[0:1, mine]
        sib, sib_decay = self.sib_total[...], self.sib_decay[0:1]
        own_first = self.core == (1 if self.back else 0)
        pick = lambda a, b: (jnp.where(own_first, a, b), jnp.where(own_first, b, a))
        return own_first, pick(own, sib), pick(own_decay, sib_decay)

    def join(self):
        for copy in self.sibling_copies():
            copy.wait_recv()
        _, (sum0, sum1), (decay0, decay1) = self.two_slabs()
        chip = decay1 * sum0 + sum1
        chip_decay = decay0 * decay1
        for lg in range(2):
            self.steps[lg] = chip_decay[:, 256 * lg : 256 * lg + 256]
            for ng in range(8):
                self.pieces[ng * 2 + lg] = chip[16 * ng : 16 * ng + 16, 256 * lg : 256 * lg + 256].astype(BF16)

    def send_pieces(self):
        def go(q):
            self.piece_copy(q, self.me).start()
            self.decay_copy(q, self.me).start()

        self.others(go)
        self.inbox[self.me] = self.pieces[self.me]
        self.decay_in[self.me] = self.steps[lax.rem(self.me, 2)]

    def prefix(self):
        def arrive(q):
            self.piece_copy(q, q).wait_recv()
            self.decay_copy(q, q).wait_recv()

        self.others(arrive)

        def step(k, state):
            q = NCHIP - 1 - k if self.back else k
            self.outbox[q] = state.astype(BF16)
            return self.decay_in[q] * state + self.inbox[q].astype(F32)

        lax.fori_loop(0, NCHIP, step, jnp.zeros((16, 256), F32))

    def send_states(self):
        self.others(lambda q: self.state_copy(q, self.me).start())
        self.landed[self.me] = self.outbox[self.me]

    def collect(self):
        self.others(lambda q: self.state_copy(q, q).wait_recv())
        own_first, (sum0, _), (decay0, _) = self.two_slabs()
        chip = jnp.concatenate(
            [jnp.concatenate([self.landed[2 * ng], self.landed[2 * ng + 1]], axis=1) for ng in range(8)], axis=0
        ).astype(F32)
        then = decay0 * chip + sum0
        self.state[self.core] = jnp.where(own_first, chip, then)
        self.away[...] = jnp.where(own_first, then, chip)
        self.back_copy().start()

    def ready(self):
        self.back_copy().wait_recv()

    def drain(self):
        def done(q):
            self.piece_copy(q, self.me).wait_send()
            self.decay_copy(q, self.me).wait_send()
            self.state_copy(q, self.me).wait_send()

        self.others(done)
        for copy in self.sibling_copies():
            copy.wait_send()
        self.back_copy().wait_send()


def scan_scratch():
    return [
        pltpu.VMEM((SPAN, 512), F32),
        pltpu.VMEM((8, 512), F32),
        pltpu.VMEM((NCHIP, 16, 256), BF16),
        pltpu.VMEM((2, 1, 256), F32),
        pltpu.VMEM((NCHIP, 16, 256), BF16),
        pltpu.VMEM((NCHIP, 1, 256), F32),
        pltpu.VMEM((NCHIP, 16, 256), BF16),
        pltpu.VMEM((NCHIP, 16, 256), BF16),
        pltpu.VMEM((SPAN, 512), F32),
        pltpu.VMEM((2, SPAN, 512), F32),
    ] + [pltpu.SemaphoreType.DMA((NCHIP,))] * 6 + [pltpu.SemaphoreType.DMA((3,))] * 2


def side_scratch():
    return [
        pltpu.VMEM((TOKENS, 128), BF16),
        pltpu.VMEM((TOKENS, 128), BF16),
        pltpu.VMEM((TOKENS, WIDE), BF16),
        pltpu.VMEM((HEADS, TOKENS), F32),
        pltpu.VMEM((HEADS, TOKENS), F32),
        pltpu.VMEM((HEADS, TOKENS), F32),
        pltpu.VMEM((TOKENS, WIDE), F32),
        pltpu.VMEM((SPAN, WIDE), F32),
        pltpu.VMEM((8, WIDE), F32),
        pltpu.VMEM((SPAN, WIDE), F32),
        pltpu.VMEM((8, WIDE), F32),
    ]


N_SIDE, N_SCAN = 11, 18
LAST = {0: (1,), 1: (0, 2)}


def kernel(hid, x_in, seg_next, pbc_in, pdt_in, bias_in, rate_in, skip_in, bc_in, dt_in, seg_prev, g_in,
           next_out, back_out, *rest):
    next_refs, rest = rest[:N_SIDE], rest[N_SIDE:]
    back_refs, rest = rest[:N_SIDE], rest[N_SIDE:]
    next_scan_refs, rest = rest[:N_SCAN], rest[N_SCAN:]
    back_scan_refs, rest = rest[:N_SCAN], rest[N_SCAN:]
    (seg_n, seg_p, pbc, taps_in, pdt, bias_row, rate_row, skip_row, column, rate_col, skip_col,
     wbuf, ptmp, hbuf, acc, dts, bc_send, bc_recv, dt_recv, next_res, back_res,
     in_sem, hid_sem, out_sem, a2a_send, a2a_recv, ring_send, ring_recv, pair_send, pair_recv) = rest

    z, xl, c, xh, y = place()
    me = z * 4 + xl * 2 + c
    chip = z * 2 + xl
    half = lax.rem(y, 2)
    y_pair = y + 1 - 2 * half
    group = xh * 2 + y // 2
    heads_first = (xh * 4 + y) * HEADS
    own_in_group = xh == half
    other_x, other_c = 1 - xl, 1 - c
    barrier = pltpu.get_barrier_semaphore()

    def greet(**where):
        pl.semaphore_signal(barrier, inc=1, device_id=where, device_id_type=MESH)

    def meet(d, carry):
        greet(**chip_id(lax.rem(chip + d, NCHIP)))
        return carry

    lax.fori_loop(1, NCHIP, meet, 0)
    greet(c=other_c)
    greet(y=y_pair)
    for src in range(4):
        @pl.when(jnp.logical_not(own_in_group & (y == src)))
        def _():
            greet(xh=half, y=jnp.int32(src))

    b_lanes = pl.ds(pl.multiple_of(group * 128, 128), 128)
    c_lanes = pl.ds(pl.multiple_of(group * 128 + 512, 128), 128)
    loads = {}
    for k, (name, src, dst) in enumerate((
        ("taps", pdt_in, taps_in), ("pbc", pbc_in, pbc),
        ("rate", rate_in, rate_row), ("skip", skip_in, skip_row), ("bias", bias_in, bias_row),
        ("seg_p", seg_prev, seg_p), ("seg_n", seg_next, seg_n),
        ("dt", dt_in, back_refs[3]), ("b", bc_in.at[:, b_lanes], back_refs[0]), ("c", bc_in.at[:, c_lanes], back_refs[1]),
        ("g", g_in, back_refs[2]), ("x", x_in, next_refs[2]),
    )):
        loads[name] = pltpu.make_async_copy(src, dst, in_sem.at[k])
        loads[name].start()

    def hid_copy(j):
        lanes = pl.ds(pl.multiple_of(256 * j + 128 * half, 128), 128)
        return pltpu.make_async_copy(
            hid.at[:, lanes], hbuf.at[:, pl.ds(pl.multiple_of(128 * j, 128), 128)], hid_sem.at[j])

    def load_hid(j, carry):
        hid_copy(j).start()
        return carry

    lax.fori_loop(0, NSLAB, load_hid, 0)

    loads["taps"].wait()
    lane_class = iota((32, 128), 1) >> 5
    taps = taps_in[...].astype(F32)
    for g in range(4):
        turned = pltpu.roll(taps, lax.rem(32 * (y - g) + 128, 128), 1)
        mine = jnp.where(lane_class == y, turned, 0.0).astype(BF16)
        pdt[g, :, 0:128] = mine[0:16]
        pdt[g, :, 128:256] = mine[16:32]
    for name in ("rate", "skip", "bias", "seg_p", "seg_n", "pbc"):
        loads[name].wait()
    rate_col[...] = per_head_column(rate_row[...], column, heads_first)
    skip_col[...] = per_head_column(skip_row[...], column, heads_first)
    bias_col = per_head_column(bias_row[...], column, heads_first)[:, 0:1]
    nxt = Side(False, next_refs, me * TOKENS, bounds_of(seg_n), rate_col, skip_col)
    back = Side(True, back_refs, me * TOKENS, bounds_of(seg_p), rate_col, skip_col)
    nxt_scan = Scan(False, chip, c, nxt.total, nxt.decay, next_scan_refs)
    back_scan = Scan(True, chip, c, back.total, back.decay, back_scan_refs)


    @pl.when(own_in_group)
    def _():
        pl.semaphore_wait(barrier, NCHIP - 1 + 2 + 3)

    @pl.when(jnp.logical_not(own_in_group))
    def _():
        pl.semaphore_wait(barrier, NCHIP - 1 + 2 + 4)


    my_rows = pl.ds(pl.multiple_of(32 * y, 32), 32)

    def spread_copies(g, source, where):
        rows = pl.ds(pl.multiple_of(32 * source, 32), 32)
        parts = ((pbc.at[:, pl.ds(128 * g, 128)], wbuf.at[me, rows, pl.ds(0, 128)]),
                 (pbc.at[:, pl.ds(512 + 128 * g, 128)], wbuf.at[me, rows, pl.ds(128, 128)]),
                 (pdt.at[g], ptmp.at[source]))
        return [
            pltpu.make_async_remote_copy(
                src, dst, a2a_send.at[g, k], a2a_recv.at[source, k], device_id=where, device_id_type=MESH)
            for k, (src, dst) in enumerate(parts)
        ]

    def spread(g):
        to_y = 2 * (g % 2) + xh
        mine = (xh == g // 2) & (y == to_y)
        return mine, spread_copies(g, y, {"xh": jnp.int32(g // 2), "y": to_y})

    for g in range(4):
        mine, copies = spread(g)

        @pl.when(jnp.logical_not(mine))
        def _():
            for copy in copies:
                copy.start()

        @pl.when(mine)
        def _():
            wbuf[me, my_rows, 0:128] = pbc[:, 128 * g : 128 * g + 128]
            wbuf[me, my_rows, 128:256] = pbc[:, 512 + 128 * g : 512 + 128 * g + 128]
            ptmp[y] = pdt[g]

    for name in ("dt", "b", "c", "g"):
        loads[name].wait()
    back.summarize()
    back_scan.share()

    for src in range(4):
        @pl.when(jnp.logical_not(own_in_group & (y == src)))
        def _():
            for copy in spread_copies(0, src, {"xh": half, "y": jnp.int32(src)}):
                copy.wait_recv()

    packed = (ptmp[0].astype(F32) + ptmp[1].astype(F32)) + (ptmp[2].astype(F32) + ptmp[3].astype(F32))
    wbuf[me, 128:144, :] = packed.astype(BF16)

    right, left = lax.rem(z + 1, NZ), lax.rem(z + NZ - 1, NZ)
    ROWS = (pl.ds(0, 64), pl.ds(64, 80))
    sends = []

    def forward(slot, chunk, **where):
        part = wbuf.at[slot, ROWS[chunk]]
        copy = pltpu.make_async_remote_copy(
            part, part, ring_send.at[len(sends)], ring_recv.at[slot, chunk],
            device_id=where, device_id_type=MESH)
        copy.start()
        sends.append(copy)

    def arrive(slot, chunk):
        part = wbuf.at[slot, ROWS[chunk]]
        pltpu.make_async_remote_copy(
            part, part, ring_send.at[0], ring_recv.at[slot, chunk],
            device_id={"z": right}, device_id_type=MESH).wait_recv()

    def multiply_group(hop):
        def multiply(i, carry):
            if hop in (0, 4):
                oz, ox = lax.rem(z + hop, NZ), i
            else:
                oz, ox = lax.rem(z + NZ - hop + (i // 2) * (2 * hop), NZ), lax.rem(i, 2)
            j = oz * 2 + ox
            for chunk in (0, 1):
                arrive(2 * j + other_c, chunk)
            hid_copy(2 * j).wait()
            hid_copy(2 * j + 1).wait()
            columns = hbuf[:, pl.ds(pl.multiple_of(256 * j, 256), 256)]
            weights, parts = [], []
            for k in (2 * j, 2 * j + 1):
                weights.append(wbuf[k, 0:128, :])
                low = wbuf[k, 128:144, :].astype(F32)
                block = jnp.concatenate([low[:, 0:128], low[:, 128:256]], axis=0)
                parts += [jnp.where(lane_class == q, block, 0.0) for q in range(4)]
            acc[:, 0:256] += dot(columns, jnp.concatenate(weights, axis=0), 1, 0)
            acc[:, 256:384] += dot(columns, jnp.concatenate(parts, axis=0).astype(BF16), 1, 0)
            return carry

        lax.fori_loop(0, 2 if hop in (0, 4) else 4, multiply, 0)

    mate = me + 2 - 4 * xl
    for chunk in (0, 1):
        forward(me, chunk, z=right)
        forward(me, chunk, z=left)
        forward(me, chunk, xl=other_x)
    for chunk in (0, 1):
        forward(me, chunk, c=other_c)
    acc[...] = jnp.zeros_like(acc)
    back.within()
    arrive(mate, 0)
    forward(mate, 0, z=right)
    forward(mate, 0, z=left)
    forward(mate, 0, c=other_c)
    late = [mate]
    for hop in range(1, 5):
        fresh = []
        for chunk in (0, 1, 2):
            for side in (0, 1):
                if hop == 4 and chunk not in LAST[side]:
                    continue
                oz = lax.rem(z + NZ - hop, NZ) if side == 0 else lax.rem(z + hop, NZ)
                column_slot = oz * 4 + xl * 2 + c
                across = oz * 4 + other_x * 2 + c
                slot, part = (across, 0) if chunk == 2 else (column_slot, chunk)
                arrive(slot, part)
                if hop < 3 or (hop == 3 and chunk in LAST[side]):
                    forward(slot, part, z=right if side == 0 else left)
                if chunk == 1:
                    forward(slot, 1, xl=other_x)
                    fresh.append(across)
                forward(slot, part, c=other_c)
        for slot in late:
            arrive(slot, 1)
            forward(slot, 1, c=other_c)
        late = fresh
        if hop == 3:
            back_scan.join()
            back_scan.send_pieces()
        multiply_group(hop - 1)
    for slot in late:
        arrive(slot, 1)
        forward(slot, 1, c=other_c)
    multiply_group(4)

    folded = acc[:, 256:384].T
    dts[...] = (folded[0:32] + folded[32:64]) + (folded[64:96] + folded[96:128])
    bc_send[...] = acc[:, 0:256].astype(BF16)
    their_heads = pl.ds(pl.multiple_of(16 - 16 * half, 16), 16)
    pair = [
        pltpu.make_async_remote_copy(
            src, dst, pair_send.at[k], pair_recv.at[k], device_id={"y": y_pair}, device_id_type=MESH)
        for k, (src, dst) in enumerate(((dts.at[their_heads], dt_recv), (bc_send, bc_recv)))
    ]
    for copy in pair:
        copy.start()
    for copy in pair:
        copy.wait_recv()
    total = acc[:, 0:256] + bc_recv[...].astype(F32)
    nxt.bv[...] = total[:, 0:128].astype(BF16)
    nxt.cv[...] = total[:, 128:256].astype(BF16)
    v = dts[pl.ds(pl.multiple_of(16 * half, 16), 16)] + dt_recv[...] + bias_col
    nxt.dt[...] = jnp.maximum(v, 0.0) + jnp.log1p(jnp.exp(-jnp.abs(v)))
    loads["x"].wait()
    nxt.summarize()
    nxt_scan.share()
    back_scan.prefix()
    nxt_scan.join()
    nxt_scan.send_pieces()
    back_scan.send_states()
    nxt.within()
    nxt_scan.prefix()
    nxt_scan.send_states()
    back_scan.collect()
    back_scan.ready()
    back.finish(back_scan.state, back_res)
    back_write = pltpu.make_async_copy(back_res, back_out, out_sem.at[0])
    back_write.start()
    nxt_scan.collect()
    nxt_scan.ready()
    nxt.finish(nxt_scan.state, next_res)
    next_write = pltpu.make_async_copy(next_res, next_out, out_sem.at[1])
    next_write.start()
    for g in range(4):
        mine, copies = spread(g)

        @pl.when(jnp.logical_not(mine))
        def _():
            for copy in copies:
                copy.wait_send()

    for copy in sends:
        copy.wait_send()
    for copy in pair:
        copy.wait_send()
    back_scan.drain()
    nxt_scan.drain()
    back_write.wait()
    next_write.wait()


def body(hidden_next, values_next, seg_next, proj_bc, proj_dt, dt_bias, decay_rate, skip_gain,
         bc_prev, dt_prev, seg_prev, grad_prev):
    as_row = lambda a: a.reshape(1, 128)
    out = jax.ShapeDtypeStruct((TOKENS, WIDE), BF16)
    dma = pltpu.SemaphoreType.DMA
    return pl.pallas_call(
        kernel,
        out_shape=(out, out),
        in_specs=[ANY] * 12,
        out_specs=(ANY, ANY),
        scratch_shapes=side_scratch() + side_scratch() + scan_scratch() + scan_scratch() + [
            pltpu.SMEM((4,), I32),
            pltpu.SMEM((4,), I32),
            pltpu.VMEM((32, 1024), BF16),
            pltpu.VMEM((32, 128), BF16),
            pltpu.VMEM((4, 16, 256), BF16),
            pltpu.VMEM((1, 128), F32),
            pltpu.VMEM((1, 128), F32),
            pltpu.VMEM((1, 128), F32),
            pltpu.VMEM((128, 128), F32),
            pltpu.VMEM((HEADS, 128), F32),
            pltpu.VMEM((HEADS, 128), F32),
            pltpu.VMEM((NSLAB, 144, 256), BF16),
            pltpu.VMEM((4, 16, 256), BF16),
            pltpu.VMEM((TOKENS, 4096), BF16),
            pltpu.VMEM((TOKENS, 384), F32),
            pltpu.VMEM((32, TOKENS), F32),
            pltpu.VMEM((TOKENS, 256), BF16),
            pltpu.VMEM((TOKENS, 256), BF16),
            pltpu.VMEM((HEADS, TOKENS), F32),
            pltpu.VMEM((TOKENS, WIDE), BF16),
            pltpu.VMEM((TOKENS, WIDE), BF16),
            dma((12,)), dma((NSLAB,)), dma((2,)), dma((4, 3)), dma((4, 3)), dma((62,)), dma((NSLAB, 2)), dma((2,)), dma((2,)),
        ],
        compiler_params=pltpu.CompilerParams(
            vmem_limit_bytes=62 << 20, collective_id=0, has_side_effects=True),
        name="layer",
    )(hidden_next, values_next, seg_next, proj_bc, proj_dt, as_row(dt_bias), as_row(decay_rate), as_row(skip_gain),
      bc_prev, dt_prev.T, seg_prev, grad_prev)


def solution(mesh):
    split = Mesh(mesh.devices.reshape(8, 2, 2, 2, 4), ("z", "xl", "c", "xh", "y"))
    tokens, both, rows = P(SEQ, None), P(SEQ, FSDP), P(SEQ + FSDP, None)
    in_specs = (tokens, both, P(), rows, rows, P(), P(), P(), tokens, both, P(), both)
    return jax.shard_map(body, mesh=split, in_specs=in_specs, out_specs=(both, both), check_vma=False)
```

time: 90.8 us -> 69.4 us (0.76)
  Pallas kernels: 81 us -> 64.8 us
  local copies, waits for them, and re-layouts: 8.62 us -> 3.74 us
    pallas_call x5 -> x1, Pallas kernels: 81 us -> 64.8 us  [body(): pl.pallas_call(kernel, out_shape=(out, out), in_specs=[ANY] * 12, out_spe...]
    unnamed x27 -> x2, local copies, waits for them, and re-layouts: 8.62 us -> 3.74 us
where the time goes in v2:
time: 69.4 us; the launch traced here: 69.2 us
  Pallas kernels  64.8 us (93%)
  local copies, waits for them, and re-layouts  3.74 us (5%)
    pallas_call x1, Pallas kernels, body(): pl.pallas_call(kernel, out_shape=(out, out), in_specs=[ANY] * 12, out_spe...  64.8 us
    unnamed x2, local copies, waits for them, and re-layouts  3.74 us

profile of v2, /device:TPU:1, one launch (start us, length us, event | category | flops | bytes accessed | tf_op | source)
XLA Modules:
  0.0 69.2 jit_solution(2891766941555894866)
XLA Ops:
  0.6 64.8 %layer.1 = (bf16[256,1024]{1,0:T(8,128)(2,1)}, bf16[256,1024]{1,0:T(8,128)(2,1)}) custom-call(bf16[256,8192]{1,0:T(8,128)(2,1)} %hid.1, bf16[256,1024]{1,0:T(8,128)(2,1)} %x_in.1, s32[4]{0:T(128)} %seg_next.1, bf16[32,1024]{1,0:T(8,128)(2,1)} %pbc_in.1, bf16[32,128]{1,0:T(8,128)(2,1)} %pdt_in.1, f32[1,128]{1,0:T(1,128)} %bitcast.5, f32[1,128]{1,0:T(1,128)} %bitcast.6, ...), custom_call_target="tpu_custom_call" | custom-call | tf_op jit(solution)/shard_map/layer/pallas_call | solution.py:604
  65.5 1.9 %copy.16 = bf16[256,1024]{1,0:T(8,128)(2,1)} copy(bf16[256,1024]{1,0:T(8,128)(2,1)} %get-tuple-element.4) | data formatting | bytes 1048576
  67.3 1.9 %copy.17 = bf16[256,1024]{1,0:T(8,128)(2,1)} copy(bf16[256,1024]{1,0:T(8,128)(2,1)} %get-tuple-element.5) | data formatting | bytes 1048576
